TPU v7x, 32 devices: a whole 2x2x4 slice. The times are simulated.
32 devices in a mesh: row: 8 (over z, y), col: 4 (over x, core).
Axes of the slice: x: 2, y: 2, z: 4, core: 2. Of those that a mesh axis runs over, the one named last changes fastest.
Arguments:
- act_quant: bfloat16 [512, 8192], P('row', 'col'), may hold values from -127 to 127, as said below
- act_scale: float32 [512], replicated, may hold values from 0.004 to 0.04
- gate_up_quant: bfloat16 [2, 8192, 29568], P(None, 'col', 'row'), may hold values from -127 to 127, as said below
- gate_up_scale: float32 [2, 29568], P(None, 'row'), may hold values from 5e-05 to 0.0005
- down_quant: bfloat16 [29568, 8192], P('row', 'col'), may hold values from -127 to 127, as said below
- down_scale: float32 [8192], P('col'), may hold values from 3e-05 to 0.0003
Outputs:
- mixed_out: bfloat16 [512, 8192], P('row', 'col')
Inputs may be any that keep to these rules, and one draw needn't show every extreme that they name: `act_quant`: whole numbers. `gate_up_quant`: whole numbers. `down_quant`: whole numbers.
All inputs are finite; a program needn't handle non-finite values.
Results may differ from a plain program's by a relative error of at most 0.005.
Values may be sent and summed in bfloat16 or wider, within the bound.
A program may use at most 128 MiB of HBM per device.

v0:
```python
import jax
import jax.numpy as jnp
from jax import lax
from jax.sharding import PartitionSpec as P


def body(act_quant, act_scale, gate_up_quant, gate_up_scale, down_quant, down_scale):
    feature_width = gate_up_quant.shape[2]
    gathered = lax.all_gather(act_quant, "row", axis=0, tiled=True)
    share_rows = gathered.shape[0] // lax.axis_size("col")
    gate_part = jnp.dot(gathered, gate_up_quant[0], preferred_element_type=jnp.float32)
    up_part = jnp.dot(gathered, gate_up_quant[1], preferred_element_type=jnp.float32)
    summed = lax.psum_scatter(
        jnp.concatenate([gate_part, up_part], axis=1), "col", scatter_dimension=0, tiled=True
    )
    token_scale = lax.dynamic_slice_in_dim(
        act_scale, lax.axis_index("col") * share_rows, share_rows, 0
    )
    gate_val = summed[:, :feature_width] * token_scale[:, None] * gate_up_scale[0][None, :]
    up_val = summed[:, feature_width:] * token_scale[:, None] * gate_up_scale[1][None, :]
    hidden = (jax.nn.silu(gate_val) * up_val).astype(jnp.bfloat16)
    hidden = lax.all_gather(hidden, "col", axis=0, tiled=True)
    mixed_out = lax.psum_scatter(
        jnp.dot(hidden, down_quant, preferred_element_type=jnp.float32) * down_scale[None, :],
        "row",
        scatter_dimension=0,
        tiled=True,
    )
    return mixed_out.astype(jnp.bfloat16)


def solution(mesh):
    in_specs = (
        P("row", "col"),
        P(),
        P(None, "col", "row"),
        P(None, "row"),
        P("row", "col"),
        P("col"),
    )
    out_specs = P("row", "col")
    return jax.shard_map(body, mesh=mesh, in_specs=in_specs, out_specs=out_specs, check_vma=False)
```

profile of v0, /device:TPU:0, one launch (start us, length us, event | category | flops | bytes accessed | tf_op | source)
XLA Modules:
  0.0 351.1 jit_solution(16619677064941690027)
XLA Ops:
  6.5 0.0 all-gather.3.cloned.1.call-start
  6.5 0.7 all-gather.3.cloned.1.call-update
  7.3 0.0 reduce-scatter.3.cloned.1.call-start
  7.3 54.0 %all-gather.3.cloned.1.call-done = bf16[512,2048]{1,0:T(8,128)(2,1)} async-done(((bf16[64,2048]{1,0:T(8,128)(2,1)}), bf16[512,2048]{1,0:T(8,128)(2,1)}) %all-gather.3.cloned.1.call-update) | async-done | bytes 2097168 | tf_op jit(solution)/shard_map/all_gather | solution.py:9
  61.3 11.8 %fusion = f32[512,3696]{0,1:T(8,128)S(1)} fusion(bf16[512,2048]{1,0:T(8,128)(2,1)} %all-gather.3.cloned.1.call-done, bf16[2,2048,3696]{1,2,0:T(8,128)(2,1)} %param.8), kind=kOutput, calls=%fused_computation.1 | convolution fusion | flops 7751073792 | bytes 24805376 | tf_op jit(solution)/shard_map/dot_general | solution.py:12
  73.1 11.8 %fusion.2 = f32[512,3696]{0,1:T(8,128)S(1)} fusion(bf16[512,2048]{1,0:T(8,128)(2,1)} %all-gather.3.cloned.1.call-done, bf16[2,2048,3696]{1,2,0:T(8,128)(2,1)} %param.8), kind=kOutput, calls=%fused_computation.3 | convolution fusion | flops 7751073792 | bytes 24805376 | tf_op jit(solution)/shard_map/dot_general | solution.py:11
  84.9 6.2 %pad_maximum_fusion = f32[512,7392]{0,1:T(8,128)} fusion(f32[512,3696]{0,1:T(8,128)S(1)} %fusion, f32[512,3696]{0,1:T(8,128)S(1)} %fusion.2), kind=kLoop, calls=%fused_computation | loop fusion | flops 3784704 | bytes 30277632 | tf_op jit(solution)/shard_map/concatenate | solution.py:14
  91.2 0.0 copy-start
  91.2 0.0 reduce-scatter.3.cloned.1.call-update
  91.2 0.0 copy-start.1
  91.2 0.0 all-gather.5.cloned.1.call-start
  91.3 0.8 dynamic_slice.3
  92.0 0.0 copy-done
  92.0 0.1 slice_reduce_fusion.1
  92.1 110.6 %reduce-scatter.3.cloned.1.call-done = f32[128,7392]{0,1:T(8,128)} async-done(((f32[512,7392]{0,1:T(8,128)}), f32[128,7392]{0,1:T(8,128)}) %reduce-scatter.3.cloned.1.call-update) | async-done | bytes 3784720 | tf_op jit(solution)/shard_map/reduce_scatter | solution.py:13
  202.7 4.8 %fusion.8 = bf16[128,3696]{0,1:T(8,128)(2,1)} fusion(f32[128,7392]{0,1:T(8,128)} %reduce-scatter.3.cloned.1.call-done, f32[3696]{0:T(1024)S(1)} %get-tuple-element.6, f32[3696]{0:T(1024)S(1)} %get-tuple-element.5, f32[128]{0:T(128)S(1)} %dynamic_slice.3), kind=kLoop, calls=%fused_computation.11 | loop fusion | flops 4730880 | bytes 4760960 | tf_op jit(solution)/shard_map/convert_element_type | solution.py:21
  207.5 0.0 all-gather.5.cloned.1.call-update
  207.5 0.0 reduce-scatter.5.cloned.1.call-start
  207.6 32.7 %all-gather.5.cloned.1.call-done = bf16[512,3696]{0,1:T(8,128)(2,1)} async-done(((bf16[128,3696]{0,1:T(8,128)(2,1)}), bf16[512,3696]{0,1:T(8,128)(2,1)}) %all-gather.5.cloned.1.call-update) | async-done | bytes 3784720 | tf_op jit(solution)/shard_map/all_gather | solution.py:22
  240.3 0.0 copy-done.1
  240.3 14.1 %convolution_multiply_fusion = f32[512,2048]{1,0:T(8,128)} fusion(bf16[512,3696]{0,1:T(8,128)(2,1)} %all-gather.5.cloned.1.call-done, bf16[3696,2048]{1,0:T(8,128)(2,1)} %param.10, f32[2048]{0:T(1024)S(1)} %copy-done.1), kind=kOutput, calls=%fused_computation.7 | convolution fusion | flops 7752122368 | bytes 23126016 | tf_op jit(solution)/shard_map/dot_general | solution.py:24
  254.4 0.0 reduce-scatter.5.cloned.1.call-update
  254.4 88.4 %reduce-scatter.5.cloned.1.call-done = f32[64,2048]{1,0:T(8,128)} async-done(((f32[512,2048]{1,0:T(8,128)}), f32[64,2048]{1,0:T(8,128)}) %reduce-scatter.5.cloned.1.call-update) | async-done | bytes 524304 | tf_op jit(solution)/shard_map/reduce_scatter | solution.py:23
  342.8 1.8 convert_element_type.7
Async XLA Ops:
  6.5 54.8 %all-gather.3.cloned.1.call-start = ((), (), s32[]{:S(2)}) async-start(), calls=%async_computation.2 | async-start | bytes 2359296 | tf_op jit(solution)/shard_map/all_gather | solution.py:9
  7.3 195.5 %reduce-scatter.3.cloned.1.call-start = ((), (), s32[]{:S(2)}) async-start(), calls=%async_computation.3 | async-start | bytes 18923520 | tf_op jit(solution)/shard_map/reduce_scatter | solution.py:13
  91.2 0.9 copy-start
  91.2 149.1 %copy-start.1 = (f32[2048]{0:T(1024)S(1)}, f32[2048]{0:T(1024)}, u32[]{:S(2)}) copy-start(f32[2048]{0:T(1024)} %param.11) | copy-start | bytes 24580
  91.2 149.1 %all-gather.5.cloned.1.call-start = ((), (), s32[]{:S(2)}) async-start(), calls=%async_computation.4 | async-start | bytes 4730880 | tf_op jit(solution)/shard_map/all_gather | solution.py:22
  207.5 135.3 %reduce-scatter.5.cloned.1.call-start = ((), (), s32[]{:S(2)}) async-start(), calls=%async_computation.5 | async-start | bytes 4718592 | tf_op jit(solution)/shard_map/reduce_scatter | solution.py:23
Sparse Core Ops, SparseCore 0:
  9.5 51.7 all-gather.2
  91.3 111.3 reduce-scatter.2
  207.7 32.6 all-gather.4
  254.5 88.2 reduce-scatter.4
where the time goes:
time: 351 us
  waiting for transfers between devices  287 us (82%)
  matrix products  37.7 us (11%)
  between operations  13.2 us (4%)
  other arithmetic  12.8 us (4%)
    reduce_scatter x1, waiting for transfers between devices, body(): lax.psum_scatter(jnp.concatenate([gate_part, up_part], axis=1), 'col', sc...  111 us
    reduce_scatter x1, waiting for transfers between devices, body(): lax.psum_scatter(jnp.dot(hidden, down_quant, preferred_element_type=jnp.f...  88.4 us
    all_gather x1, waiting for transfers between devices, body(): gathered = lax.all_gather(act_quant, 'row', axis=0, tiled=True)  54 us
    all_gather x1, waiting for transfers between devices, body(): hidden = lax.all_gather(hidden, 'col', axis=0, tiled=True)  32.7 us
    dot_general x1, matrix products, body(): jnp.dot(hidden, down_quant, preferred_element_type=jnp.float32)  14.1 us
    dot_general x1, matrix products, body(): jnp.dot(gathered, gate_up_quant[0], preferred_element_type=jnp.float32)  11.8 us
    dot_general x1, matrix products, body(): jnp.dot(gathered, gate_up_quant[1], preferred_element_type=jnp.float32)  11.8 us
  transfers between devices with their start and end apart: 4, of which 4 were waited for; matrix products, arithmetic and copies ran while one was open for 0% of the time, Pallas kernels for 0%

commit v1 on v0

--- a/solution.py
+++ b/solution.py
@@ -1,12 +1,36 @@
+import functools
 import jax
 import jax.numpy as jnp
 from jax import lax
 from jax.sharding import PartitionSpec as P
 
 
+def press_space(field, mesh_ax):
+    slots = lax.axis_size(mesh_ax)
+    v_now = range(slots)
+    val2 = map(lambda k0: (k0, (k0 + 1) % slots), v_now)
+    found = list(val2)
+
+    def map_the_views(after):
+        if len(after) == slots:
+            return after
+        w2 = lax.ppermute(after[0], mesh_ax, found)
+        all_values = map_the_views([w2, *after])
+        return all_values
+
+    now = map_the_views([field])
+    response = jnp.concatenate(now, 0)
+    outcome_arr = lax.axis_index(mesh_ax)
+    a_now = jnp.roll(response, (outcome_arr + 1) * field.shape[0], 0)
+    return a_now
+
+
+_bring_slots = functools.partial(press_space, mesh_ax="row")
+
+
 def body(act_quant, act_scale, gate_up_quant, gate_up_scale, down_quant, down_scale):
     feature_width = gate_up_quant.shape[2]
-    gathered = lax.all_gather(act_quant, "row", axis=0, tiled=True)
+    gathered = _bring_slots(act_quant)
     share_rows = gathered.shape[0] // lax.axis_size("col")
     gate_part = jnp.dot(gathered, gate_up_quant[0], preferred_element_type=jnp.float32)
     up_part = jnp.dot(gathered, gate_up_quant[1], preferred_element_type=jnp.float32)

time: 351 us -> 382 us (1.088)
  local copies, waits for them, and re-layouts: 0.85 us -> 13.3 us
  waiting for transfers between devices: 287 us -> 296 us
    ppermute x0 -> x7, waiting for transfers between devices: none -> 66 us  [map_the_views(): w2 = lax.ppermute(after[0], mesh_ax, found)]
    all_gather x1 -> x0, waiting for transfers between devices: 54 us -> none  [body(): gathered = lax.all_gather(act_quant, 'row', axis=0, tiled=True)]
    unnamed x4 -> x21, local copies, waits for them, and re-layouts: 0.01 us -> 11.8 us
  transfers between devices with their start and end apart: 4 -> 10, of which waited for: 4 -> 10; matrix products, arithmetic and copies ran while one was open for 0% -> 0% of each run, Pallas kernels for 0% -> 0%
where the time goes in v1:
time: 382 us
  waiting for transfers between devices  296 us (77%)
  matrix products  39.7 us (10%)
  other arithmetic  15.9 us (4%)
  local copies, waits for them, and re-layouts  13.3 us (3%)
  between operations  13.2 us (3%)
    reduce_scatter x1, waiting for transfers between devices, body(): lax.psum_scatter(jnp.concatenate([gate_part, up_part], axis=1), 'col', sc...  109 us
    reduce_scatter x1, waiting for transfers between devices, body(): lax.psum_scatter(jnp.dot(hidden, down_quant, preferred_element_type=jnp.f...  88.5 us
    ppermute x7, waiting for transfers between devices, map_the_views(): w2 = lax.ppermute(after[0], mesh_ax, found)  66 us
    all_gather x1, waiting for transfers between devices, body(): hidden = lax.all_gather(hidden, 'col', axis=0, tiled=True)  32.5 us
    dot_general x1, matrix products, body(): jnp.dot(hidden, down_quant, preferred_element_type=jnp.float32)  14.1 us
    dot_general x1, matrix products, body(): jnp.dot(gathered, gate_up_quant[1], preferred_element_type=jnp.float32)  14 us
    unnamed x21, local copies, waits for them, and re-layouts  11.8 us
    dot_general x1, matrix products, body(): jnp.dot(gathered, gate_up_quant[0], preferred_element_type=jnp.float32)  11.6 us
  transfers between devices with their start and end apart: 10, of which 10 were waited for; matrix products, arithmetic and copies ran while one was open for 0% of the time, Pallas kernels for 0%

profile of v1, /device:TPU:0, one launch (start us, length us, event | category | flops | bytes accessed | tf_op | source)
XLA Modules:
  0.0 381.7 jit_solution(9686658294118683427)
XLA Ops:
  6.5 0.0 reduce-scatter.3.cloned.1.call-start
  6.5 3.0 collective-permute-start
  9.5 9.6 %collective-permute-done = bf16[64,2048]{1,0:T(8,128)(2,1)S(1)} collective-permute-done((bf16[64,2048]{1,0:T(8,128)(2,1)}, bf16[64,2048]{1,0:T(8,128)(2,1)S(1)}, u32[]{:S(2)}, u32[]{:S(2)}) %collective-permute-start) | collective-permute-done | bytes 262176 | tf_op jit(solution)/shard_map/ppermute | solution.py:17
  19.2 0.0 collective-permute-start.1
  19.2 10.2 %collective-permute-done.1 = bf16[64,2048]{1,0:T(8,128)(2,1)S(1)} collective-permute-done((bf16[64,2048]{1,0:T(8,128)(2,1)S(1)}, bf16[64,2048]{1,0:T(8,128)(2,1)S(1)}, u32[]{:S(2)}, u32[]{:S(2)}) %collective-permute-start.1) | collective-permute-done | bytes 262176 | tf_op jit(solution)/shard_map/ppermute | solution.py:17
  29.3 0.0 collective-permute-start.2
  29.3 9.3 %collective-permute-done.2 = bf16[64,2048]{1,0:T(8,128)(2,1)S(1)} collective-permute-done((bf16[64,2048]{1,0:T(8,128)(2,1)S(1)}, bf16[64,2048]{1,0:T(8,128)(2,1)S(1)}, u32[]{:S(2)}, u32[]{:S(2)}) %collective-permute-start.2) | collective-permute-done | bytes 262176 | tf_op jit(solution)/shard_map/ppermute | solution.py:17
  38.6 0.0 collective-permute-start.3
  38.6 9.1 %collective-permute-done.3 = bf16[64,2048]{1,0:T(8,128)(2,1)S(1)} collective-permute-done((bf16[64,2048]{1,0:T(8,128)(2,1)S(1)}, bf16[64,2048]{1,0:T(8,128)(2,1)S(1)}, u32[]{:S(2)}, u32[]{:S(2)}) %collective-permute-start.3) | collective-permute-done | bytes 262176 | tf_op jit(solution)/shard_map/ppermute | solution.py:17
  47.7 0.0 collective-permute-start.4
  47.7 9.1 %collective-permute-done.4 = bf16[64,2048]{1,0:T(8,128)(2,1)S(1)} collective-permute-done((bf16[64,2048]{1,0:T(8,128)(2,1)S(1)}, bf16[64,2048]{1,0:T(8,128)(2,1)S(1)}, u32[]{:S(2)}, u32[]{:S(2)}) %collective-permute-start.4) | collective-permute-done | bytes 262176 | tf_op jit(solution)/shard_map/ppermute | solution.py:17
  56.8 0.0 collective-permute-start.5
  56.8 9.7 %collective-permute-done.5 = bf16[64,2048]{1,0:T(8,128)(2,1)S(1)} collective-permute-done((bf16[64,2048]{1,0:T(8,128)(2,1)S(1)}, bf16[64,2048]{1,0:T(8,128)(2,1)S(1)}, u32[]{:S(2)}, u32[]{:S(2)}) %collective-permute-start.5) | collective-permute-done | bytes 262176 | tf_op jit(solution)/shard_map/ppermute | solution.py:17
  66.5 0.0 collective-permute-start.6
  66.5 9.1 %collective-permute-done.6 = bf16[64,2048]{1,0:T(8,128)(2,1)S(1)} collective-permute-done((bf16[64,2048]{1,0:T(8,128)(2,1)S(1)}, bf16[64,2048]{1,0:T(8,128)(2,1)S(1)}, u32[]{:S(2)}, u32[]{:S(2)}) %collective-permute-start.6) | collective-permute-done | bytes 262176 | tf_op jit(solution)/shard_map/ppermute | solution.py:17
  75.5 0.7 constant_dynamic-update-slice_fusion.15
  76.2 0.7 constant_dynamic-update-slice_fusion.14
  77.0 0.7 constant_dynamic-update-slice_fusion.13
  77.7 0.7 constant_dynamic-update-slice_fusion.12
  78.4 0.7 constant_dynamic-update-slice_fusion.11
  79.1 0.7 constant_dynamic-update-slice_fusion.10
  79.9 0.7 constant_dynamic-update-slice_fusion.9
  80.6 1.7 constant_dynamic-update-slice_fusion.8
  82.3 0.7 constant_dynamic-update-slice_fusion.7
  83.0 0.7 constant_dynamic-update-slice_fusion.6
  83.7 0.7 constant_dynamic-update-slice_fusion.5
  84.4 0.7 constant_dynamic-update-slice_fusion.4
  85.1 0.7 constant_dynamic-update-slice_fusion.3
  85.9 0.7 constant_dynamic-update-slice_fusion.2
  86.6 0.7 constant_dynamic-update-slice_fusion.1
  87.3 0.7 constant_dynamic-update-slice_fusion
  88.0 11.6 %fusion.2 = f32[512,3696]{0,1:T(8,128)S(1)} fusion(bf16[2,2048,3696]{1,2,0:T(8,128)(2,1)} %param.8, bf16[1024,2048]{1,0:T(8,128)(2,1)} %constant_dynamic-update-slice_fusion, s32[]{:T(128)S(6)} %select_n.17), kind=kOutput, calls=%fused_computation.3 | convolution fusion | flops 7751073792 | bytes 24805380 | tf_op jit(solution)/shard_map/dot_general | solution.py:35
  99.7 14.0 %fusion = f32[512,3696]{0,1:T(8,128)} fusion(bf16[2,2048,3696]{1,2,0:T(8,128)(2,1)} %param.8, bf16[1024,2048]{1,0:T(8,128)(2,1)} %constant_dynamic-update-slice_fusion, s32[]{:T(128)S(6)} %select_n.17), kind=kOutput, calls=%fused_computation.1 | convolution fusion | flops 7751073792 | bytes 24805380 | tf_op jit(solution)/shard_map/dot_general | solution.py:36
  113.6 9.4 %pad_maximum_fusion = f32[512,7392]{0,1:T(8,128)} fusion(f32[512,3696]{0,1:T(8,128)} %fusion, f32[512,3696]{0,1:T(8,128)S(1)} %fusion.2), kind=kLoop, calls=%fused_computation | loop fusion | flops 3784704 | bytes 30277632 | tf_op jit(solution)/shard_map/concatenate | solution.py:38
  123.0 0.0 reduce-scatter.3.cloned.1.call-update
  123.0 0.0 copy-start.2
  123.0 0.0 all-gather.2.cloned.1.call-start
  123.1 0.8 dynamic_slice.8
  123.8 0.1 slice_reduce_fusion.1
  123.9 109.2 %reduce-scatter.3.cloned.1.call-done = f32[128,7392]{0,1:T(8,128)} async-done(((f32[512,7392]{0,1:T(8,128)}), f32[128,7392]{0,1:T(8,128)}) %reduce-scatter.3.cloned.1.call-update) | async-done | bytes 3784720 | tf_op jit(solution)/shard_map/reduce_scatter | solution.py:37
  233.1 4.8 %fusion.8 = bf16[128,3696]{0,1:T(8,128)(2,1)} fusion(f32[128,7392]{0,1:T(8,128)} %reduce-scatter.3.cloned.1.call-done, f32[3696]{0:T(1024)S(1)} %get-tuple-element.6, f32[3696]{0:T(1024)S(1)} %get-tuple-element.5, f32[128]{0:T(128)S(1)} %dynamic_slice.8), kind=kLoop, calls=%fused_computation.11 | loop fusion | flops 4730880 | bytes 4760960 | tf_op jit(solution)/shard_map/convert_element_type | solution.py:45
  237.9 0.0 all-gather.2.cloned.1.call-update
  237.9 0.2 reduce-scatter.5.cloned.1.call-start
  238.2 32.5 %all-gather.2.cloned.1.call-done = bf16[512,3696]{0,1:T(8,128)(2,1)} async-done(((bf16[128,3696]{0,1:T(8,128)(2,1)}), bf16[512,3696]{0,1:T(8,128)(2,1)}) %all-gather.2.cloned.1.call-update) | async-done | bytes 3784720 | tf_op jit(solution)/shard_map/all_gather | solution.py:46
  270.7 14.1 %convolution_multiply_fusion = f32[512,2048]{1,0:T(8,128)} fusion(bf16[512,3696]{0,1:T(8,128)(2,1)} %all-gather.2.cloned.1.call-done, bf16[3696,2048]{1,0:T(8,128)(2,1)} %param.10, f32[2048]{0:T(1024)S(1)} %copy-done.2), kind=kOutput, calls=%fused_computation.7 | convolution fusion | flops 7752122368 | bytes 23126016 | tf_op jit(solution)/shard_map/dot_general | solution.py:48
  284.9 0.0 reduce-scatter.5.cloned.1.call-update
  284.9 88.5 %reduce-scatter.5.cloned.1.call-done = f32[64,2048]{1,0:T(8,128)} async-done(((f32[512,2048]{1,0:T(8,128)}), f32[64,2048]{1,0:T(8,128)}) %reduce-scatter.5.cloned.1.call-update) | async-done | bytes 524304 | tf_op jit(solution)/shard_map/reduce_scatter | solution.py:47
  373.4 1.8 convert_element_type.7
  (5 shorter events, 0.0 us)
Async XLA Ops:
  6.5 80.8 %copy-start = (bf16[64,2048]{1,0:T(8,128)(2,1)S(1)}, bf16[64,2048]{1,0:T(8,128)(2,1)}, u32[]{:S(2)}) copy-start(bf16[64,2048]{1,0:T(8,128)(2,1)} %param.6) | copy-start | bytes 786436
  6.5 226.6 %reduce-scatter.3.cloned.1.call-start = ((), (), s32[]{:S(2)}) async-start(), calls=%async_computation.2 | async-start | bytes 18923520 | tf_op jit(solution)/shard_map/reduce_scatter | solution.py:37
  6.5 12.6 %collective-permute-start = (bf16[64,2048]{1,0:T(8,128)(2,1)}, bf16[64,2048]{1,0:T(8,128)(2,1)S(1)}, u32[]{:S(2)}, u32[]{:S(2)}) collective-permute-start(bf16[64,2048]{1,0:T(8,128)(2,1)} %param.6), channel_id=1, source_target_pairs={{0,4},{4,8},{8,12},{12,16},{16,20},{20,24},{24,28},{28,0},{1,5},{5... | collective-permute-start | bytes 786440 | tf_op jit(solution)/shard_map/ppermute | solution.py:17
  19.2 10.2 %collective-permute-start.1 = (bf16[64,2048]{1,0:T(8,128)(2,1)S(1)}, bf16[64,2048]{1,0:T(8,128)(2,1)S(1)}, u32[]{:S(2)}, u32[]{:S(2)}) collective-permute-start(bf16[64,2048]{1,0:T(8,128)(2,1)S(1)} %collective-permute-done), channel_id=1, source_target_pairs={{0,4},{4,8},{8,12},{12,16},{16,20},{20,24},{24,28},{28,0},{1,5},{5... | collective-permute-start | bytes 786440 | tf_op jit(solution)/shard_map/ppermute | solution.py:17
  29.3 9.3 %collective-permute-start.2 = (bf16[64,2048]{1,0:T(8,128)(2,1)S(1)}, bf16[64,2048]{1,0:T(8,128)(2,1)S(1)}, u32[]{:S(2)}, u32[]{:S(2)}) collective-permute-start(bf16[64,2048]{1,0:T(8,128)(2,1)S(1)} %collective-permute-done.1), channel_id=1, source_target_pairs={{0,4},{4,8},{8,12},{12,16},{16,20},{20,24},{24,28},{28,0},{1,5},{5... | collective-permute-start | bytes 786440 | tf_op jit(solution)/shard_map/ppermute | solution.py:17
  38.6 9.1 %collective-permute-start.3 = (bf16[64,2048]{1,0:T(8,128)(2,1)S(1)}, bf16[64,2048]{1,0:T(8,128)(2,1)S(1)}, u32[]{:S(2)}, u32[]{:S(2)}) collective-permute-start(bf16[64,2048]{1,0:T(8,128)(2,1)S(1)} %collective-permute-done.2), channel_id=1, source_target_pairs={{0,4},{4,8},{8,12},{12,16},{16,20},{20,24},{24,28},{28,0},{1,5},{5... | collective-permute-start | bytes 786440 | tf_op jit(solution)/shard_map/ppermute | solution.py:17
  47.7 9.1 %collective-permute-start.4 = (bf16[64,2048]{1,0:T(8,128)(2,1)S(1)}, bf16[64,2048]{1,0:T(8,128)(2,1)S(1)}, u32[]{:S(2)}, u32[]{:S(2)}) collective-permute-start(bf16[64,2048]{1,0:T(8,128)(2,1)S(1)} %collective-permute-done.3), channel_id=1, source_target_pairs={{0,4},{4,8},{8,12},{12,16},{16,20},{20,24},{24,28},{28,0},{1,5},{5... | collective-permute-start | bytes 786440 | tf_op jit(solution)/shard_map/ppermute | solution.py:17
  56.8 9.7 %collective-permute-start.5 = (bf16[64,2048]{1,0:T(8,128)(2,1)S(1)}, bf16[64,2048]{1,0:T(8,128)(2,1)S(1)}, u32[]{:S(2)}, u32[]{:S(2)}) collective-permute-start(bf16[64,2048]{1,0:T(8,128)(2,1)S(1)} %collective-permute-done.4), channel_id=1, source_target_pairs={{0,4},{4,8},{8,12},{12,16},{16,20},{20,24},{24,28},{28,0},{1,5},{5... | collective-permute-start | bytes 786440 | tf_op jit(solution)/shard_map/ppermute | solution.py:17
  66.5 9.1 %collective-permute-start.6 = (bf16[64,2048]{1,0:T(8,128)(2,1)S(1)}, bf16[64,2048]{1,0:T(8,128)(2,1)S(1)}, u32[]{:S(2)}, u32[]{:S(2)}) collective-permute-start(bf16[64,2048]{1,0:T(8,128)(2,1)S(1)} %collective-permute-done.5), channel_id=1, source_target_pairs={{0,4},{4,8},{8,12},{12,16},{16,20},{20,24},{24,28},{28,0},{1,5},{5... | collective-permute-start | bytes 786440 | tf_op jit(solution)/shard_map/ppermute | solution.py:17
  123.0 0.9 copy-start.1
  123.0 147.7 %copy-start.2 = (f32[2048]{0:T(1024)S(1)}, f32[2048]{0:T(1024)}, u32[]{:S(2)}) copy-start(f32[2048]{0:T(1024)} %param.11) | copy-start | bytes 24580
  123.0 147.7 %all-gather.2.cloned.1.call-start = ((), (), s32[]{:S(2)}) async-start(), calls=%async_computation.3 | async-start | bytes 4730880 | tf_op jit(solution)/shard_map/all_gather | solution.py:46
  237.9 135.4 %reduce-scatter.5.cloned.1.call-start = ((), (), s32[]{:S(2)}) async-start(), calls=%async_computation.4 | async-start | bytes 4718592 | tf_op jit(solution)/shard_map/reduce_scatter | solution.py:47
Sparse Core Ops, SparseCore 0:
  123.1 109.9 reduce-scatter.2
  238.1 32.6 all-gather.1
  285.0 88.3 reduce-scatter.4
